TPU v7x, 32 devices: a whole 2x2x4 slice. The times are simulated.
32 devices in a mesh: cluster: 8 (over z, y), sub: 4 (over x, core).
Axes of the slice: x: 2, y: 2, z: 4, core: 2. Of those that a mesh axis runs over, the one named last changes fastest.
Arguments:
- rhs: float32 [128, 4, 384], P(('cluster', 'sub')), may hold values from -8 to 8
- operators: bfloat16 [128, 384, 384], P(('cluster', 'sub')), may hold values from -1 to 5
- signs: int32 [128, 384], P(('cluster', 'sub')), may hold values from -1 to 1, as said below
- links: int32 [128, 3, 128], P(('cluster', 'sub')), may hold values from 0 to 127, as said below
- cluster_basis: float32 [128, 24, 384], P(('cluster', 'sub')), may hold values from -0.3125 to 0.3125
- corner_basis: float32 [128, 8, 384], P(('cluster', 'sub')), may hold values from -0.3125 to 0.3125
- corner_ids: int32 [128, 8], P(('cluster', 'sub')), may hold values from 0 to 127
- cluster_coarse: float32 [8, 384, 384], P('cluster', 'sub'), may hold values from -1 to 3
- global_coarse: float32 [128, 128], P('sub'), may hold values from -0.2 to 0.5
Outputs:
- multipliers: float32 [128, 4, 384], P(('cluster', 'sub'))
- residual: float32 [128, 4, 384], P(('cluster', 'sub'))
Inputs may be any that keep to these rules, and one draw needn't show every extreme that they name: `signs`: each entry is -1 or 1. Each links[s, b] is a permutation of 0 to 127; both subdomains of an interface pair hold the same permutation for it.
All inputs are finite; a program needn't handle non-finite values.
Results may differ from a plain program's by a relative error of at most 0.007.
Values sent between devices are 32-bit elements; how exact they have to be, the bound alone decides.
A program may use at most 64 MiB of HBM per device.

v0:
```python
import jax
import jax.numpy as jnp
from jax import lax
from jax.sharding import PartitionSpec as P

ITERS = 2
HIGHEST_PRECISION = lax.Precision.HIGHEST


def extended(block, sides, width):
    for axis, dim in sides:
        count = lax.axis_size(axis)
        forward = [(i, i + 1) for i in range(count - 1)]
        backward = [(target, source) for source, target in forward]
        low = lax.ppermute(
            lax.slice_in_dim(block, block.shape[dim] - width, None, axis=dim), axis, forward
        )
        high = lax.ppermute(lax.slice_in_dim(block, 0, width, axis=dim), axis, backward)
        block = jnp.concatenate([low, block, high], axis=dim)
    return block


def invert(order):
    row_index = jnp.broadcast_to(jnp.arange(order.shape[0], dtype=jnp.int32)[:, None], order.shape)
    col_index = jnp.broadcast_to(jnp.arange(order.shape[1], dtype=jnp.int32)[None, :], order.shape)
    return jnp.zeros_like(order).at[row_index, order].set(col_index)


def permuted(blocks, order):
    return jnp.take_along_axis(blocks, order[:, None, :], axis=2)


def interface(vector, tables):
    inv_up, order_down, inv_even, order_odd = tables
    block_width = vector.shape[2] // 3
    up_part = vector[:, :, :block_width]
    down_part = vector[:, :, block_width : 2 * block_width]
    across = vector[:, :, 2 * block_width :]
    send_up = permuted(up_part, inv_up)
    send_down = permuted(down_part, order_down)
    inside_rims = extended(jnp.stack([send_down, send_up]), (("sub", 0),), 1)
    send_even = permuted(across[0::2], inv_even)
    send_odd = permuted(across[1::2], order_odd)
    outside_rims = extended(jnp.stack([send_odd, send_even]), (("cluster", 0),), 1)
    new_across = jnp.stack([outside_rims[3], outside_rims[0]], axis=1).reshape(across.shape)
    return jnp.concatenate([inside_rims[3], inside_rims[0], new_across], axis=2)


def apply(vector, sign_field, operators, tables):
    spread = sign_field * (vector + interface(vector, tables))
    product = jnp.einsum(
        "srk,skl->srl", spread.astype(jnp.bfloat16), operators, preferred_element_type=jnp.float32
    )
    curvature = lax.psum(jnp.sum(spread * product, axis=(0, 2)), ("cluster", "sub"))
    signed = sign_field * product
    result = signed + interface(signed, tables)
    return (result, curvature)


def project(vector, coarse):
    cluster_basis, corner_basis, flat_ids, onehot, cluster_coarse, global_coarse = coarse
    load_count = vector.shape[1]
    local_subs = vector.shape[0]
    cluster_coef = jnp.einsum("srl,skl->srk", vector, cluster_basis, precision=HIGHEST_PRECISION)
    own_coef = cluster_coef.transpose(1, 0, 2).reshape(load_count, -1)
    part_cluster = jnp.dot(own_coef, cluster_coarse[0], precision=HIGHEST_PRECISION)
    corner_coef = jnp.einsum(
        "scl,srl->rsc", corner_basis, vector, precision=HIGHEST_PRECISION
    ).reshape(load_count, -1)
    corner_local = jnp.dot(corner_coef, onehot, precision=HIGHEST_PRECISION)
    squares = jnp.sum(vector * vector, axis=(0, 2))
    row_count = global_coarse.shape[0]
    corner_whole, total_norm = lax.psum((corner_local, squares), ("cluster", "sub"))
    corner_rows = lax.dynamic_slice_in_dim(
        corner_whole, lax.axis_index("sub") * row_count, row_count, 1
    )
    part_global = jnp.dot(corner_rows, global_coarse, precision=HIGHEST_PRECISION)
    cluster_all, global_all = lax.psum((part_cluster, part_global), "sub")
    own_width = own_coef.shape[1]
    cluster_own = lax.dynamic_slice_in_dim(
        cluster_all, lax.axis_index("sub") * own_width, own_width, 1
    )
    cluster_own = cluster_own.reshape(load_count, local_subs, -1)
    fix_cluster = jnp.einsum(
        "rsk,skl->srl", cluster_own, cluster_basis, precision=HIGHEST_PRECISION
    )
    picked = jnp.take(global_all, flat_ids, axis=1).reshape(load_count, local_subs, -1)
    fix_corner = jnp.einsum("rsc,scl->srl", picked, corner_basis, precision=HIGHEST_PRECISION)
    return (vector - fix_cluster - fix_corner, total_norm)


def local(
    rhs,
    operators,
    signs,
    links,
    cluster_basis,
    corner_basis,
    corner_ids,
    cluster_coarse,
    global_coarse,
):
    sign_field = signs.astype(jnp.float32)[:, None, :]
    tables = (invert(links[:, 0]), links[:, 1], invert(links[0::2, 2]), links[1::2, 2])
    flat_ids = corner_ids.reshape(-1)
    onehot = (
        flat_ids[:, None] == jnp.arange(global_coarse.shape[1], dtype=jnp.int32)[None, :]
    ).astype(jnp.float32)
    coarse = (cluster_basis, corner_basis, flat_ids, onehot, cluster_coarse, global_coarse)
    residual = rhs
    projected, residual_norm = project(residual, coarse)
    direction = projected
    multipliers = jnp.zeros_like(rhs)
    for iteration in range(ITERS):
        product, curvature = apply(direction, sign_field, operators, tables)
        step_size = (residual_norm / curvature)[None, :, None]
        multipliers = multipliers + step_size * direction
        residual = residual - step_size * product
        if iteration + 1 < ITERS:
            projected, norm_next = project(residual, coarse)
            direction = projected + (norm_next / residual_norm)[None, :, None] * direction
            residual_norm = norm_next
    return (multipliers, residual)


def solution(mesh):
    placed = (
        P(("cluster", "sub"), None, None),
        P(("cluster", "sub"), None, None),
        P(("cluster", "sub"), None),
        P(("cluster", "sub"), None, None),
        P(("cluster", "sub"), None, None),
        P(("cluster", "sub"), None, None),
        P(("cluster", "sub"), None),
        P("cluster", "sub", None),
        P("sub", None),
    )
    return jax.shard_map(
        local,
        mesh=mesh,
        in_specs=placed,
        out_specs=(P(("cluster", "sub"), None, None), P(("cluster", "sub"), None, None)),
        check_vma=False,
    )
```

profile of v0, /device:TPU:1, one launch (start us, length us, event | category | flops | bytes accessed | tf_op | source)
XLA Modules:
  0.0 322.6 jit_solution(7329631267407565892)
XLA Ops:
  0.7 0.9 eq.15
  1.5 0.7 slice.78
  2.3 1.2 convolution_bitcast_fusion.3
  3.6 1.0 convolution_bitcast_fusion.2
  4.7 0.2 fusion.16
  4.9 40.5 %psum.72 = f32[4,128]{1,0:T(4,128)S(1)} all-reduce(f32[4,128]{1,0:T(4,128)S(1)} %fusion.16), channel_id=1, replica_groups=mesh['cluster'=8,'sub'=4] {'cluster','sub'}, use_global_device_ids=true, to_apply=%region_3.0 | all-reduce | flops 512 | bytes 4096 | tf_op jit(solution)/shard_map/psum | solution.py:73
  45.4 1.1 fusion.3
  46.5 0.9 fusion.46
  47.4 7.2 %all-reduce.3 = (f32[4,384]{1,0:T(4,128)S(1)}, f32[4,128]{1,0:T(4,128)S(1)}) all-reduce(f32[4,384]{1,0:T(4,128)S(1)} %fusion.3, f32[4,128]{1,0:T(4,128)S(1)} %fusion.46), channel_id=1, replica_groups=mesh['cluster'=8,'sub'=4] {'sub'}, use_global_device_ids=true, to_apply=%region_2.0 | all-reduce | flops 2048 | bytes 16384 | tf_op jit(solution)/shard_map/psum | solution.py:78
  54.8 1.1 convolution_subtract_fusion.3
  56.0 0.6 gather_fusion
  56.6 1.1 convolution_subtract_fusion.2
  57.9 1.9 gather_fusion.3
  59.9 1.3 collective-permute-start.2
  61.2 11.4 %scatter_fusion.1 = s32[2,128]{1,0:T(2,128)S(1)} fusion(s32[2,128]{1,0:T(2,128)S(1)} %broadcast.105, s32[256]{0:T(256)S(1)} %fusion.53, s32[256]{0:T(256)S(1)} %iota_bitcast_fusion.1), kind=kCustom, calls=%fused_computation.19 | custom fusion | bytes 5120 | tf_op jit(solution)/shard_map/scatter | solution.py:26
  72.9 1.9 gather_fusion.4
  74.9 4.0 %collective-permute-start.3 = (f32[1,2,4,128]{3,2,1,0:T(4,128)S(1)}, f32[1,2,4,128]{3,2,1,0:T(4,128)S(1)}, u32[]{:S(2)}, u32[]{:S(2)}) collective-permute-start(f32[1,2,4,128]{3,2,1,0:T(4,128)S(1)} %select_bitcast_fusion.6), channel_id=1, source_target_pairs={{0,4},{4,8},{8,12},{12,16},{16,20},{20,24},{24,28},{1,5},{5,9},{9,... | collective-permute-start | bytes 12296 | tf_op jit(solution)/shard_map/ppermute | solution.py:15
  79.0 3.7 %gather_fusion.1 = f32[512,4]{1,0:T(8,128)S(1)} fusion(f32[4,4,128]{1,2,0:T(8,128)S(1)} %copy.49, s32[512]{0:T(512)S(1)} %get-tuple-element.39), kind=kCustom, calls=%fused_computation.1.clone | custom fusion | bytes 20480 | tf_op jit(solution)/shard_map/jit(take_along_axis)/gather | solution.py:30
  82.8 3.1 collective-permute-start
  86.0 22.5 %scatter_fusion = s32[4,128]{1,0:T(4,128)S(1)} fusion(s32[4,128]{1,0:T(4,128)S(1)} %broadcast.103, s32[512]{0:T(512)S(1)} %get-tuple-element.40, s32[512]{0:T(512)S(1)} %iota_bitcast_fusion), kind=kCustom, calls=%fused_computation.18 | custom fusion | bytes 10240 | tf_op jit(solution)/shard_map/scatter | solution.py:26
  108.7 3.7 %gather_fusion.2 = f32[512,4]{1,0:T(8,128)S(1)} fusion(f32[4,4,128]{1,2,0:T(8,128)S(1)} %copy.51, s32[512]{0:T(512)S(1)} %fusion.40), kind=kCustom, calls=%fused_computation.4.clone | custom fusion | bytes 20480 | tf_op jit(solution)/shard_map/jit(take_along_axis)/gather | solution.py:30
  112.5 3.3 %collective-permute-start.1 = (f32[1,4,4,128]{3,2,1,0:T(4,128)S(1)}, f32[1,4,4,128]{3,2,1,0:T(4,128)S(1)}, u32[]{:S(2)}, u32[]{:S(2)}) collective-permute-start(f32[1,4,4,128]{3,2,1,0:T(4,128)S(1)} %fusion.27), channel_id=1, source_target_pairs={{0,1},{1,2},{2,3},{4,5},{5,6},{6,7},{8,9},{9,10},{10,11},{12,13},{... | collective-permute-start | bytes 24584 | tf_op jit(solution)/shard_map/ppermute | solution.py:15
  116.0 0.6 collective-permute-done.1
  116.6 0.4 multiply_reduce_fusion.2
  117.2 1.9 gather_fusion.7
  119.1 1.3 collective-permute-start.6
  120.6 1.9 gather_fusion.8
  122.6 4.4 %collective-permute-start.7 = (f32[1,2,4,128]{3,2,1,0:T(4,128)S(1)}, f32[1,2,4,128]{3,2,1,0:T(4,128)S(1)}, u32[]{:S(2)}, u32[]{:S(2)}) collective-permute-start(f32[1,2,4,128]{3,2,1,0:T(4,128)S(1)} %select_bitcast_fusion.4), channel_id=1, source_target_pairs={{0,4},{4,8},{8,12},{12,16},{16,20},{20,24},{24,28},{1,5},{5,9},{9,... | collective-permute-start | bytes 12296 | tf_op jit(solution)/shard_map/ppermute | solution.py:15
  127.2 3.7 %gather_fusion.5 = f32[512,4]{1,0:T(8,128)S(1)} fusion(f32[4,4,128]{1,2,0:T(8,128)S(1)} %copy.57, s32[512]{0:T(512)S(1)} %get-tuple-element.39), kind=kCustom, calls=%fused_computation.5.clone | custom fusion | bytes 20480 | tf_op jit(solution)/shard_map/jit(take_along_axis)/gather | solution.py:30
  131.0 2.4 collective-permute-start.4
  133.5 3.7 %gather_fusion.6 = f32[512,4]{1,0:T(8,128)S(1)} fusion(f32[4,4,128]{1,2,0:T(8,128)S(1)} %copy.59, s32[512]{0:T(512)S(1)} %fusion.40), kind=kCustom, calls=%fused_computation.6.clone | custom fusion | bytes 20480 | tf_op jit(solution)/shard_map/jit(take_along_axis)/gather | solution.py:30
  137.3 4.2 %collective-permute-start.5 = (f32[1,4,4,128]{3,2,1,0:T(4,128)S(1)}, f32[1,4,4,128]{3,2,1,0:T(4,128)S(1)}, u32[]{:S(2)}, u32[]{:S(2)}) collective-permute-start(f32[1,4,4,128]{3,2,1,0:T(4,128)S(1)} %fusion.25), channel_id=1, source_target_pairs={{0,1},{1,2},{2,3},{4,5},{5,6},{6,7},{8,9},{9,10},{10,11},{12,13},{... | collective-permute-start | bytes 24584 | tf_op jit(solution)/shard_map/ppermute | solution.py:15
  141.5 39.1 %all-reduce.1 = (f32[4]{0:T(128)S(1)}, f32[4]{0:T(128)S(1)}) all-reduce(f32[4]{0:T(128)S(1)} %multiply_reduce_fusion.3, f32[4]{0:T(128)S(1)} %get-tuple-element.17), channel_id=1, replica_groups=mesh['cluster'=8,'sub'=4] {'cluster','sub'}, use_global_device_ids=true, to_apply=%region_1.0 | all-reduce | flops 8 | bytes 64 | tf_op jit(solution)/shard_map/psum | solution.py:73
  180.7 0.2 multiply_reduce_fusion.1
  181.1 0.3 convolution_bitcast_fusion.1
  181.5 0.2 fusion.15
  181.7 38.6 %all-reduce = (f32[4,128]{1,0:T(4,128)S(1)}, f32[4]{0:T(128)S(1)}) all-reduce(f32[4,128]{1,0:T(4,128)S(1)} %fusion.15, f32[4]{0:T(128)S(1)} %get-tuple-element.13), channel_id=1, replica_groups=mesh['cluster'=8,'sub'=4] {'cluster','sub'}, use_global_device_ids=true, to_apply=%region_12.16 | all-reduce | flops 516 | bytes 4128 | tf_op jit(solution)/shard_map/psum | solution.py:73
  220.3 0.2 fusion.44
  220.6 0.2 fusion.1
  220.8 7.2 %all-reduce.2 = (f32[4,384]{1,0:T(4,128)S(1)}, f32[4,128]{1,0:T(4,128)S(1)}) all-reduce(f32[4,384]{1,0:T(4,128)S(1)} %fusion.1, f32[4,128]{1,0:T(4,128)S(1)} %fusion.44), channel_id=1, replica_groups=mesh['cluster'=8,'sub'=4] {'sub'}, use_global_device_ids=true, to_apply=%region_11.15 | all-reduce | flops 2048 | bytes 16384 | tf_op jit(solution)/shard_map/psum | solution.py:78
  228.2 0.2 convolution_subtract_fusion.1
  228.5 0.6 gather_fusion.9
  229.1 0.3 fusion
  229.6 1.9 gather_fusion.12
  231.6 1.3 collective-permute-start.10
  233.0 1.9 gather_fusion.13
  235.0 4.1 %collective-permute-start.11 = (f32[1,2,4,128]{3,2,1,0:T(4,128)S(1)}, f32[1,2,4,128]{3,2,1,0:T(4,128)S(1)}, u32[]{:S(2)}, u32[]{:S(2)}) collective-permute-start(f32[1,2,4,128]{3,2,1,0:T(4,128)S(1)} %select_bitcast_fusion.2), channel_id=1, source_target_pairs={{0,4},{4,8},{8,12},{12,16},{16,20},{20,24},{24,28},{1,5},{5,9},{9,... | collective-permute-start | bytes 12296 | tf_op jit(solution)/shard_map/ppermute | solution.py:15
  239.3 3.7 %gather_fusion.10 = f32[512,4]{1,0:T(8,128)S(1)} fusion(f32[4,4,128]{1,2,0:T(8,128)S(1)} %copy.71, s32[512]{0:T(512)S(1)} %get-tuple-element.39), kind=kCustom, calls=%fused_computation.7.clone | custom fusion | bytes 20480 | tf_op jit(solution)/shard_map/jit(take_along_axis)/gather | solution.py:30
  243.1 3.7 %collective-permute-start.8 = (f32[1,4,4,128]{3,2,1,0:T(4,128)S(1)}, f32[1,4,4,128]{3,2,1,0:T(4,128)S(1)}, u32[]{:S(2)}, u32[]{:S(2)}) collective-permute-start(f32[1,4,4,128]{3,2,1,0:T(4,128)S(1)} %fusion.24), channel_id=1, source_target_pairs={{1,0},{2,1},{3,2},{5,4},{6,5},{7,6},{9,8},{10,9},{11,10},{13,12},{... | collective-permute-start | bytes 24584 | tf_op jit(solution)/shard_map/ppermute | solution.py:18
  246.9 3.7 %gather_fusion.11 = f32[512,4]{1,0:T(8,128)S(1)} fusion(f32[4,4,128]{1,2,0:T(8,128)S(1)} %copy.73, s32[512]{0:T(512)S(1)} %fusion.40), kind=kCustom, calls=%fused_computation.8.clone | custom fusion | bytes 20480 | tf_op jit(solution)/shard_map/jit(take_along_axis)/gather | solution.py:30
  250.7 2.6 collective-permute-start.9
  253.3 0.7 collective-permute-done.9
  254.1 0.4 broadcast_multiply_fusion
  254.5 41.2 %psum.79 = f32[4]{0:T(128)S(1)} all-reduce(f32[4]{0:T(128)S(1)} %get-tuple-element.16), channel_id=1, replica_groups=mesh['cluster'=8,'sub'=4] {'cluster','sub'}, use_global_device_ids=true, to_apply=%region_15.19 | all-reduce | flops 4 | bytes 32 | tf_op jit(solution)/shard_map/psum | solution.py:54
  295.8 1.9 gather_fusion.16
  297.8 1.5 collective-permute-start.14
  299.5 1.9 gather_fusion.17
  301.4 4.0 %collective-permute-start.15 = (f32[1,2,4,128]{3,2,1,0:T(4,128)S(1)}, f32[1,2,4,128]{3,2,1,0:T(4,128)S(1)}, u32[]{:S(2)}, u32[]{:S(2)}) collective-permute-start(f32[1,2,4,128]{3,2,1,0:T(4,128)S(1)} %select_bitcast_fusion), channel_id=1, source_target_pairs={{0,4},{4,8},{8,12},{12,16},{16,20},{20,24},{24,28},{1,5},{5,9},{9,... | collective-permute-start | bytes 12296 | tf_op jit(solution)/shard_map/ppermute | solution.py:15
  305.6 3.7 %gather_fusion.14 = f32[512,4]{1,0:T(8,128)S(1)} fusion(f32[4,4,128]{1,2,0:T(8,128)S(1)} %copy.79, s32[512]{0:T(512)S(1)} %get-tuple-element.39), kind=kCustom, calls=%fused_computation.9.clone | custom fusion | bytes 20480 | tf_op jit(solution)/shard_map/jit(take_along_axis)/gather | solution.py:30
  309.4 4.2 %collective-permute-start.12 = (f32[1,4,4,128]{3,2,1,0:T(4,128)S(1)}, f32[1,4,4,128]{3,2,1,0:T(4,128)S(1)}, u32[]{:S(2)}, u32[]{:S(2)}) collective-permute-start(f32[1,4,4,128]{3,2,1,0:T(4,128)S(1)} %fusion.22), channel_id=1, source_target_pairs={{1,0},{2,1},{3,2},{5,4},{6,5},{7,6},{9,8},{10,9},{11,10},{13,12},{... | collective-permute-start | bytes 24584 | tf_op jit(solution)/shard_map/ppermute | solution.py:18
  313.8 3.7 %gather_fusion.15 = f32[512,4]{1,0:T(8,128)S(1)} fusion(f32[4,4,128]{1,2,0:T(8,128)S(1)} %copy.81, s32[512]{0:T(512)S(1)} %fusion.40), kind=kCustom, calls=%fused_computation.10.clone | custom fusion | bytes 20480 | tf_op jit(solution)/shard_map/jit(take_along_axis)/gather | solution.py:30
  317.5 3.5 %collective-permute-start.13 = (f32[1,4,4,128]{3,2,1,0:T(4,128)S(1)}, f32[1,4,4,128]{3,2,1,0:T(4,128)S(1)}, u32[]{:S(2)}, u32[]{:S(2)}) collective-permute-start(f32[1,4,4,128]{3,2,1,0:T(4,128)S(1)} %fusion.21), channel_id=1, source_target_pairs={{0,1},{1,2},{2,3},{4,5},{5,6},{6,7},{8,9},{9,10},{10,11},{12,13},{... | collective-permute-start | bytes 24584 | tf_op jit(solution)/shard_map/ppermute | solution.py:15
  321.1 0.7 collective-permute-done.13
  321.9 0.7 fusion.10
  (126 shorter events, 5.4 us)
Async XLA Ops:
  0.6 116.0 %copy-start = (bf16[4,384,384]{2,1,0:T(8,128)(2,1)S(1)}, bf16[4,384,384]{2,1,0:T(8,128)(2,1)}, u32[]{:S(2)}) copy-start(bf16[4,384,384]{2,1,0:T(8,128)(2,1)} %param.16) | copy-start | bytes 3538948
  0.6 60.5 %copy-start.6 = (s32[4,3,128]{2,0,1:T(4,128)S(1)}, s32[4,3,128]{2,0,1:T(4,128)}, u32[]{:S(2)}) copy-start(s32[4,3,128]{2,0,1:T(4,128)} %param.18) | copy-start | bytes 18436
  59.9 56.1 %collective-permute-start.2 = (f32[1,2,4,128]{3,2,1,0:T(4,128)S(1)}, f32[1,2,4,128]{3,2,1,0:T(4,128)S(1)}, u32[]{:S(2)}, u32[]{:S(2)}) collective-permute-start(f32[1,2,4,128]{3,2,1,0:T(4,128)S(1)} %select_bitcast_fusion.7), channel_id=1, source_target_pairs={{4,0},{8,4},{12,8},{16,12},{20,16},{24,20},{28,24},{5,1},{9,5},{13... | collective-permute-start | bytes 12296 | tf_op jit(solution)/shard_map/ppermute | solution.py:18
  74.9 41.1 %collective-permute-start.3 = (f32[1,2,4,128]{3,2,1,0:T(4,128)S(1)}, f32[1,2,4,128]{3,2,1,0:T(4,128)S(1)}, u32[]{:S(2)}, u32[]{:S(2)}) collective-permute-start(f32[1,2,4,128]{3,2,1,0:T(4,128)S(1)} %select_bitcast_fusion.6), channel_id=1, source_target_pairs={{0,4},{4,8},{8,12},{12,16},{16,20},{20,24},{24,28},{1,5},{5,9},{9,... | collective-permute-start | bytes 12296 | tf_op jit(solution)/shard_map/ppermute | solution.py:15
  82.8 33.2 %collective-permute-start = (f32[1,4,4,128]{3,2,1,0:T(4,128)S(1)}, f32[1,4,4,128]{3,2,1,0:T(4,128)S(1)}, u32[]{:S(2)}, u32[]{:S(2)}) collective-permute-start(f32[1,4,4,128]{3,2,1,0:T(4,128)S(1)} %fusion.28), channel_id=1, source_target_pairs={{1,0},{2,1},{3,2},{5,4},{6,5},{7,6},{9,8},{10,9},{11,10},{13,12},{... | collective-permute-start | bytes 24584 | tf_op jit(solution)/shard_map/ppermute | solution.py:18
  85.9 29.9 %copy-start.3 = (f32[4,4,384]{2,1,0:T(4,128)S(1)}, f32[4,4,384]{2,1,0:T(4,128)}, u32[]{:S(2)}) copy-start(f32[4,4,384]{2,1,0:T(4,128)} %param.15) | copy-start | bytes 73732
  86.0 30.0 %copy-start.7 = (s32[4,384]{1,0:T(4,128)S(1)}, s32[4,384]{1,0:T(4,128)}, u32[]{:S(2)}) copy-start(s32[4,384]{1,0:T(4,128)} %param.17) | copy-start | bytes 18436
  112.5 4.1 %collective-permute-start.1 = (f32[1,4,4,128]{3,2,1,0:T(4,128)S(1)}, f32[1,4,4,128]{3,2,1,0:T(4,128)S(1)}, u32[]{:S(2)}, u32[]{:S(2)}) collective-permute-start(f32[1,4,4,128]{3,2,1,0:T(4,128)S(1)} %fusion.27), channel_id=1, source_target_pairs={{0,1},{1,2},{2,3},{4,5},{5,6},{6,7},{8,9},{9,10},{10,11},{12,13},{... | collective-permute-start | bytes 24584 | tf_op jit(solution)/shard_map/ppermute | solution.py:15
  119.1 61.5 %collective-permute-start.6 = (f32[1,2,4,128]{3,2,1,0:T(4,128)S(1)}, f32[1,2,4,128]{3,2,1,0:T(4,128)S(1)}, u32[]{:S(2)}, u32[]{:S(2)}) collective-permute-start(f32[1,2,4,128]{3,2,1,0:T(4,128)S(1)} %select_bitcast_fusion.5), channel_id=1, source_target_pairs={{4,0},{8,4},{12,8},{16,12},{20,16},{24,20},{28,24},{5,1},{9,5},{13... | collective-permute-start | bytes 12296 | tf_op jit(solution)/shard_map/ppermute | solution.py:18
  120.4 60.4 %copy-start.2 = (f32[4,8,384]{2,1,0:T(8,128)S(1)}, f32[4,8,384]{2,1,0:T(8,128)}, u32[]{:S(2)}) copy-start(f32[4,8,384]{2,1,0:T(8,128)} %param.20) | copy-start | bytes 147460
  120.6 60.5 %copy-start.1 = (f32[4,24,384]{2,1,0:T(8,128)S(1)}, f32[4,24,384]{2,1,0:T(8,128)}, u32[]{:S(2)}) copy-start(f32[4,24,384]{2,1,0:T(8,128)} %param.19) | copy-start | bytes 442372
  122.6 97.7 %copy-start.5 = (f32[32,128]{1,0:T(8,128)S(1)}, f32[32,128]{1,0:T(8,128)}, u32[]{:S(2)}) copy-start(f32[32,128]{1,0:T(8,128)} %param.23) | copy-start | bytes 49156
  122.6 98.0 %copy-start.4 = (f32[1,96,384]{2,1,0:T(8,128)S(1)}, f32[1,96,384]{2,1,0:T(8,128)}, u32[]{:S(2)}) copy-start(f32[1,96,384]{2,1,0:T(8,128)} %param.22) | copy-start | bytes 442372
  122.6 58.0 %collective-permute-start.7 = (f32[1,2,4,128]{3,2,1,0:T(4,128)S(1)}, f32[1,2,4,128]{3,2,1,0:T(4,128)S(1)}, u32[]{:S(2)}, u32[]{:S(2)}) collective-permute-start(f32[1,2,4,128]{3,2,1,0:T(4,128)S(1)} %select_bitcast_fusion.4), channel_id=1, source_target_pairs={{0,4},{4,8},{8,12},{12,16},{16,20},{20,24},{24,28},{1,5},{5,9},{9,... | collective-permute-start | bytes 12296 | tf_op jit(solution)/shard_map/ppermute | solution.py:15
  131.0 49.7 %collective-permute-start.4 = (f32[1,4,4,128]{3,2,1,0:T(4,128)S(1)}, f32[1,4,4,128]{3,2,1,0:T(4,128)S(1)}, u32[]{:S(2)}, u32[]{:S(2)}) collective-permute-start(f32[1,4,4,128]{3,2,1,0:T(4,128)S(1)} %fusion.26), channel_id=1, source_target_pairs={{1,0},{2,1},{3,2},{5,4},{6,5},{7,6},{9,8},{10,9},{11,10},{13,12},{... | collective-permute-start | bytes 24584 | tf_op jit(solution)/shard_map/ppermute | solution.py:18
  137.3 43.4 %collective-permute-start.5 = (f32[1,4,4,128]{3,2,1,0:T(4,128)S(1)}, f32[1,4,4,128]{3,2,1,0:T(4,128)S(1)}, u32[]{:S(2)}, u32[]{:S(2)}) collective-permute-start(f32[1,4,4,128]{3,2,1,0:T(4,128)S(1)} %fusion.25), channel_id=1, source_target_pairs={{0,1},{1,2},{2,3},{4,5},{5,6},{6,7},{8,9},{9,10},{10,11},{12,13},{... | collective-permute-start | bytes 24584 | tf_op jit(solution)/shard_map/ppermute | solution.py:15
  231.6 21.7 %collective-permute-start.10 = (f32[1,2,4,128]{3,2,1,0:T(4,128)S(1)}, f32[1,2,4,128]{3,2,1,0:T(4,128)S(1)}, u32[]{:S(2)}, u32[]{:S(2)}) collective-permute-start(f32[1,2,4,128]{3,2,1,0:T(4,128)S(1)} %select_bitcast_fusion.3), channel_id=1, source_target_pairs={{4,0},{8,4},{12,8},{16,12},{20,16},{24,20},{28,24},{5,1},{9,5},{13... | collective-permute-start | bytes 12296 | tf_op jit(solution)/shard_map/ppermute | solution.py:18
  235.0 18.3 %collective-permute-start.11 = (f32[1,2,4,128]{3,2,1,0:T(4,128)S(1)}, f32[1,2,4,128]{3,2,1,0:T(4,128)S(1)}, u32[]{:S(2)}, u32[]{:S(2)}) collective-permute-start(f32[1,2,4,128]{3,2,1,0:T(4,128)S(1)} %select_bitcast_fusion.2), channel_id=1, source_target_pairs={{0,4},{4,8},{8,12},{12,16},{16,20},{20,24},{24,28},{1,5},{5,9},{9,... | collective-permute-start | bytes 12296 | tf_op jit(solution)/shard_map/ppermute | solution.py:15
  243.1 10.3 %collective-permute-start.8 = (f32[1,4,4,128]{3,2,1,0:T(4,128)S(1)}, f32[1,4,4,128]{3,2,1,0:T(4,128)S(1)}, u32[]{:S(2)}, u32[]{:S(2)}) collective-permute-start(f32[1,4,4,128]{3,2,1,0:T(4,128)S(1)} %fusion.24), channel_id=1, source_target_pairs={{1,0},{2,1},{3,2},{5,4},{6,5},{7,6},{9,8},{10,9},{11,10},{13,12},{... | collective-permute-start | bytes 24584 | tf_op jit(solution)/shard_map/ppermute | solution.py:18
  250.7 3.4 %collective-permute-start.9 = (f32[1,4,4,128]{3,2,1,0:T(4,128)S(1)}, f32[1,4,4,128]{3,2,1,0:T(4,128)S(1)}, u32[]{:S(2)}, u32[]{:S(2)}) collective-permute-start(f32[1,4,4,128]{3,2,1,0:T(4,128)S(1)} %fusion.23), channel_id=1, source_target_pairs={{0,1},{1,2},{2,3},{4,5},{5,6},{6,7},{8,9},{9,10},{10,11},{12,13},{... | collective-permute-start | bytes 24584 | tf_op jit(solution)/shard_map/ppermute | solution.py:15
  297.8 23.3 %collective-permute-start.14 = (f32[1,2,4,128]{3,2,1,0:T(4,128)S(1)}, f32[1,2,4,128]{3,2,1,0:T(4,128)S(1)}, u32[]{:S(2)}, u32[]{:S(2)}) collective-permute-start(f32[1,2,4,128]{3,2,1,0:T(4,128)S(1)} %select_bitcast_fusion.1), channel_id=1, source_target_pairs={{4,0},{8,4},{12,8},{16,12},{20,16},{24,20},{28,24},{5,1},{9,5},{13... | collective-permute-start | bytes 12296 | tf_op jit(solution)/shard_map/ppermute | solution.py:18
  301.4 19.7 %collective-permute-start.15 = (f32[1,2,4,128]{3,2,1,0:T(4,128)S(1)}, f32[1,2,4,128]{3,2,1,0:T(4,128)S(1)}, u32[]{:S(2)}, u32[]{:S(2)}) collective-permute-start(f32[1,2,4,128]{3,2,1,0:T(4,128)S(1)} %select_bitcast_fusion), channel_id=1, source_target_pairs={{0,4},{4,8},{8,12},{12,16},{16,20},{20,24},{24,28},{1,5},{5,9},{9,... | collective-permute-start | bytes 12296 | tf_op jit(solution)/shard_map/ppermute | solution.py:15
  309.4 11.8 %collective-permute-start.12 = (f32[1,4,4,128]{3,2,1,0:T(4,128)S(1)}, f32[1,4,4,128]{3,2,1,0:T(4,128)S(1)}, u32[]{:S(2)}, u32[]{:S(2)}) collective-permute-start(f32[1,4,4,128]{3,2,1,0:T(4,128)S(1)} %fusion.22), channel_id=1, source_target_pairs={{1,0},{2,1},{3,2},{5,4},{6,5},{7,6},{9,8},{10,9},{11,10},{13,12},{... | collective-permute-start | bytes 24584 | tf_op jit(solution)/shard_map/ppermute | solution.py:18
  317.5 4.3 %collective-permute-start.13 = (f32[1,4,4,128]{3,2,1,0:T(4,128)S(1)}, f32[1,4,4,128]{3,2,1,0:T(4,128)S(1)}, u32[]{:S(2)}, u32[]{:S(2)}) collective-permute-start(f32[1,4,4,128]{3,2,1,0:T(4,128)S(1)} %fusion.21), channel_id=1, source_target_pairs={{0,1},{1,2},{2,3},{4,5},{5,6},{6,7},{8,9},{9,10},{10,11},{12,13},{... | collective-permute-start | bytes 24584 | tf_op jit(solution)/shard_map/ppermute | solution.py:15
where the time goes:
time: 324 us; the launch traced here: 323 us
  blocking collectives  174 us (54%)
  local copies, waits for them, and re-layouts  86 us (27%)
  starting transfers between devices  48.9 us (15%)
  matrix products  9.13 us (3%)
    psum x3, blocking collectives, project(): lax.psum((corner_local, squares), ('cluster', 'sub'))  118 us
    gather x32, local copies, waits for them, and re-layouts, permuted(): return jnp.take_along_axis(blocks, order[:, None, :], axis=2)  46 us
    psum x1, blocking collectives, apply(): lax.psum(jnp.sum(spread * product, axis=(0, 2)), ('cluster', 'sub'))  41.2 us
    scatter x2, local copies, waits for them, and re-layouts, invert(): return jnp.zeros_like(order).at[row_index, order].set(col_index)  34 us
    ppermute x8, starting transfers between devices, extended(): lax.ppermute(lax.slice_in_dim(block, block.shape[dim] - width, None, axis...  30.2 us
    ppermute x8, starting transfers between devices, extended(): lax.ppermute(lax.slice_in_dim(block, 0, width, axis=dim), axis, backward)  18.7 us
    psum x2, blocking collectives, project(): cluster_all, global_all = lax.psum((part_cluster, part_global), 'sub')  14.4 us
  transfers between devices with their start and end apart: 16, of which 3 were waited for; matrix products, arithmetic and copies ran while one was open for 23% of the time, Pallas kernels for 0%

commit v1 on v0

--- a/solution.py
+++ b/solution.py
@@ -51,7 +51,7 @@
     product = jnp.einsum(
         "srk,skl->srl", spread.astype(jnp.bfloat16), operators, preferred_element_type=jnp.float32
     )
-    curvature = lax.psum(jnp.sum(spread * product, axis=(0, 2)), ("cluster", "sub"))
+    curvature = lax.psum(lax.psum(jnp.sum(spread * product, axis=(0, 2)), "sub"), "cluster")
     signed = sign_field * product
     result = signed + interface(signed, tables)
     return (result, curvature)

time: 324 us -> 292 us (0.901)
  blocking collectives: 174 us -> 136 us
  starting transfers between devices: 48.9 us -> 54.2 us
    psum x3 -> x2, blocking collectives: 118 us -> 77.7 us  [project(): lax.psum((corner_local, squares), ('cluster', 'sub'))]
    ppermute x8, starting transfers between devices: 18.7 us -> 24.4 us  [extended(): lax.ppermute(lax.slice_in_dim(block, 0, width, axis=dim), axis, backward)]
    psum x1 -> x4, blocking collectives: 41.2 us -> 43.5 us  [the longest x2 31.4 us: apply(): lax.psum(lax.psum(jnp.sum(spread * product, axis=(0, 2)), 'sub'), 'cluster')]
  transfers between devices with their start and end apart: 16 -> 16, of which waited for: 3 -> 4; matrix products, arithmetic and copies ran while one was open for 23% -> 25% of each run, Pallas kernels for 0% -> 0%
where the time goes in v1:
time: 292 us; the launch traced here: 291 us
  blocking collectives  136 us (47%)
  local copies, waits for them, and re-layouts  86 us (29%)
  starting transfers between devices  54.2 us (19%)
  matrix products  9.14 us (3%)
    psum x2, blocking collectives, project(): lax.psum((corner_local, squares), ('cluster', 'sub'))  77.7 us
    gather x32, local copies, waits for them, and re-layouts, permuted(): return jnp.take_along_axis(blocks, order[:, None, :], axis=2)  46 us
    scatter x2, local copies, waits for them, and re-layouts, invert(): return jnp.zeros_like(order).at[row_index, order].set(col_index)  34 us
    psum x2, blocking collectives, apply(): lax.psum(lax.psum(jnp.sum(spread * product, axis=(0, 2)), 'sub'), 'cluster')  31.4 us
    ppermute x8, starting transfers between devices, extended(): lax.ppermute(lax.slice_in_dim(block, block.shape[dim] - width, None, axis...  29.8 us
    ppermute x8, starting transfers between devices, extended(): lax.ppermute(lax.slice_in_dim(block, 0, width, axis=dim), axis, backward)  24.4 us
    psum x2, blocking collectives, project(): cluster_all, global_all = lax.psum((part_cluster, part_global), 'sub')  14.4 us
    psum x2, blocking collectives, apply(): lax.psum(jnp.sum(spread * product, axis=(0, 2)), 'sub')  12.1 us
  transfers between devices with their start and end apart: 16, of which 4 were waited for; matrix products, arithmetic and copies ran while one was open for 25% of the time, Pallas kernels for 0%

profile of v1, /device:TPU:1, one launch (start us, length us, event | category | flops | bytes accessed | tf_op | source)
XLA Modules:
  0.0 291.3 jit_solution(18262869369293428800)
XLA Ops:
  0.7 0.9 eq.15
  1.5 0.7 slice.78
  2.3 0.9 multiply_reduce_fusion.3
  3.1 1.2 convolution_bitcast_fusion.3
  4.5 1.0 convolution_bitcast_fusion.2
  5.8 1.1 fusion.3
  6.9 40.5 %all-reduce.1 = (f32[4,128]{1,0:T(4,128)S(1)}, f32[4]{0:T(128)S(1)}) all-reduce(f32[4,128]{1,0:T(4,128)S(1)} %fusion.16, f32[4]{0:T(128)S(1)} %multiply_reduce_fusion.3), channel_id=1, replica_groups=mesh['cluster'=8,'sub'=4] {'cluster','sub'}, use_global_device_ids=true, to_apply=%region_3.0 | all-reduce | flops 516 | bytes 4128 | tf_op jit(solution)/shard_map/psum | solution.py:73
  47.4 0.9 fusion.46
  48.3 7.2 %all-reduce.3 = (f32[4,384]{1,0:T(4,128)S(1)}, f32[4,128]{1,0:T(4,128)S(1)}) all-reduce(f32[4,384]{1,0:T(4,128)S(1)} %fusion.3, f32[4,128]{1,0:T(4,128)S(1)} %fusion.46), channel_id=1, replica_groups=mesh['cluster'=8,'sub'=4] {'sub'}, use_global_device_ids=true, to_apply=%region_2.0 | all-reduce | flops 2048 | bytes 16384 | tf_op jit(solution)/shard_map/psum | solution.py:78
  55.6 1.1 convolution_subtract_fusion.3
  56.9 0.6 gather_fusion
  57.5 1.1 convolution_subtract_fusion.2
  58.7 1.9 gather_fusion.3
  60.7 1.3 collective-permute-start.2
  62.1 11.4 %scatter_fusion.1 = s32[2,128]{1,0:T(2,128)S(1)} fusion(s32[2,128]{1,0:T(2,128)S(1)} %broadcast.105, s32[256]{0:T(256)S(1)} %fusion.53, s32[256]{0:T(256)S(1)} %iota_bitcast_fusion.1), kind=kCustom, calls=%fused_computation.19 | custom fusion | bytes 5120 | tf_op jit(solution)/shard_map/scatter | solution.py:26
  73.7 1.9 gather_fusion.4
  75.7 4.0 %collective-permute-start.3 = (f32[1,2,4,128]{3,2,1,0:T(4,128)S(1)}, f32[1,2,4,128]{3,2,1,0:T(4,128)S(1)}, u32[]{:S(2)}, u32[]{:S(2)}) collective-permute-start(f32[1,2,4,128]{3,2,1,0:T(4,128)S(1)} %select_bitcast_fusion.6), channel_id=1, source_target_pairs={{0,4},{4,8},{8,12},{12,16},{16,20},{20,24},{24,28},{1,5},{5,9},{9,... | collective-permute-start | bytes 12296 | tf_op jit(solution)/shard_map/ppermute | solution.py:15
  79.9 3.7 %gather_fusion.1 = f32[512,4]{1,0:T(8,128)S(1)} fusion(f32[4,4,128]{1,2,0:T(8,128)S(1)} %copy.49, s32[512]{0:T(512)S(1)} %get-tuple-element.39), kind=kCustom, calls=%fused_computation.1.clone | custom fusion | bytes 20480 | tf_op jit(solution)/shard_map/jit(take_along_axis)/gather | solution.py:30
  83.7 3.1 %collective-permute-start = (f32[1,4,4,128]{3,2,1,0:T(4,128)S(1)}, f32[1,4,4,128]{3,2,1,0:T(4,128)S(1)}, u32[]{:S(2)}, u32[]{:S(2)}) collective-permute-start(f32[1,4,4,128]{3,2,1,0:T(4,128)S(1)} %fusion.28), channel_id=1, source_target_pairs={{1,0},{2,1},{3,2},{5,4},{6,5},{7,6},{9,8},{10,9},{11,10},{13,12},{... | collective-permute-start | bytes 24584 | tf_op jit(solution)/shard_map/ppermute | solution.py:18
  86.8 22.5 %scatter_fusion = s32[4,128]{1,0:T(4,128)S(1)} fusion(s32[4,128]{1,0:T(4,128)S(1)} %broadcast.103, s32[512]{0:T(512)S(1)} %get-tuple-element.40, s32[512]{0:T(512)S(1)} %iota_bitcast_fusion), kind=kCustom, calls=%fused_computation.18 | custom fusion | bytes 10240 | tf_op jit(solution)/shard_map/scatter | solution.py:26
  109.5 3.7 %gather_fusion.2 = f32[512,4]{1,0:T(8,128)S(1)} fusion(f32[4,4,128]{1,2,0:T(8,128)S(1)} %copy.51, s32[512]{0:T(512)S(1)} %fusion.40), kind=kCustom, calls=%fused_computation.4.clone | custom fusion | bytes 20480 | tf_op jit(solution)/shard_map/jit(take_along_axis)/gather | solution.py:30
  113.3 3.3 %collective-permute-start.1 = (f32[1,4,4,128]{3,2,1,0:T(4,128)S(1)}, f32[1,4,4,128]{3,2,1,0:T(4,128)S(1)}, u32[]{:S(2)}, u32[]{:S(2)}) collective-permute-start(f32[1,4,4,128]{3,2,1,0:T(4,128)S(1)} %fusion.27), channel_id=1, source_target_pairs={{0,1},{1,2},{2,3},{4,5},{5,6},{6,7},{8,9},{9,10},{10,11},{12,13},{... | collective-permute-start | bytes 24584 | tf_op jit(solution)/shard_map/ppermute | solution.py:15
  116.7 0.7 collective-permute-done.1
  117.4 0.4 multiply_reduce_fusion.2
  117.8 6.1 %psum.88 = f32[4]{0:T(128)S(1)} all-reduce(f32[4]{0:T(128)S(1)} %get-tuple-element.17), channel_id=1, replica_groups=mesh['cluster'=8,'sub'=4] {'sub'}, use_global_device_ids=true, to_apply=%region_8.12 | all-reduce | flops 4 | bytes 32 | tf_op jit(solution)/shard_map/psum | solution.py:54
  123.9 15.6 %psum.89 = f32[4]{0:T(128)S(1)} all-reduce(f32[4]{0:T(128)S(1)} %psum.88), channel_id=1, replica_groups=mesh['cluster'=8,'sub'=4] {'cluster'}, use_global_device_ids=true, to_apply=%region_9.0 | all-reduce | flops 4 | bytes 32 | tf_op jit(solution)/shard_map/psum | solution.py:54
  139.7 1.9 gather_fusion.7
  141.7 1.3 collective-permute-start.6
  143.1 1.9 gather_fusion.8
  145.1 4.3 %collective-permute-start.7 = (f32[1,2,4,128]{3,2,1,0:T(4,128)S(1)}, f32[1,2,4,128]{3,2,1,0:T(4,128)S(1)}, u32[]{:S(2)}, u32[]{:S(2)}) collective-permute-start(f32[1,2,4,128]{3,2,1,0:T(4,128)S(1)} %select_bitcast_fusion.4), channel_id=1, source_target_pairs={{0,4},{4,8},{8,12},{12,16},{16,20},{20,24},{24,28},{1,5},{5,9},{9,... | collective-permute-start | bytes 12296 | tf_op jit(solution)/shard_map/ppermute | solution.py:15
  149.6 3.7 %gather_fusion.5 = f32[512,4]{1,0:T(8,128)S(1)} fusion(f32[4,4,128]{1,2,0:T(8,128)S(1)} %copy.57, s32[512]{0:T(512)S(1)} %get-tuple-element.39), kind=kCustom, calls=%fused_computation.5.clone | custom fusion | bytes 20480 | tf_op jit(solution)/shard_map/jit(take_along_axis)/gather | solution.py:30
  153.4 6.0 %collective-permute-start.4 = (f32[1,4,4,128]{3,2,1,0:T(4,128)S(1)}, f32[1,4,4,128]{3,2,1,0:T(4,128)S(1)}, u32[]{:S(2)}, u32[]{:S(2)}) collective-permute-start(f32[1,4,4,128]{3,2,1,0:T(4,128)S(1)} %fusion.26), channel_id=1, source_target_pairs={{1,0},{2,1},{3,2},{5,4},{6,5},{7,6},{9,8},{10,9},{11,10},{13,12},{... | collective-permute-start | bytes 24584 | tf_op jit(solution)/shard_map/ppermute | solution.py:18
  159.5 3.7 %gather_fusion.6 = f32[512,4]{1,0:T(8,128)S(1)} fusion(f32[4,4,128]{1,2,0:T(8,128)S(1)} %copy.59, s32[512]{0:T(512)S(1)} %fusion.40), kind=kCustom, calls=%fused_computation.6.clone | custom fusion | bytes 20480 | tf_op jit(solution)/shard_map/jit(take_along_axis)/gather | solution.py:30
  163.3 3.6 %collective-permute-start.5 = (f32[1,4,4,128]{3,2,1,0:T(4,128)S(1)}, f32[1,4,4,128]{3,2,1,0:T(4,128)S(1)}, u32[]{:S(2)}, u32[]{:S(2)}) collective-permute-start(f32[1,4,4,128]{3,2,1,0:T(4,128)S(1)} %fusion.25), channel_id=1, source_target_pairs={{0,1},{1,2},{2,3},{4,5},{5,6},{6,7},{8,9},{9,10},{10,11},{12,13},{... | collective-permute-start | bytes 24584 | tf_op jit(solution)/shard_map/ppermute | solution.py:15
  167.0 0.7 collective-permute-done.5
  168.1 0.3 convolution_bitcast_fusion.1
  168.6 37.3 %all-reduce = (f32[4,128]{1,0:T(4,128)S(1)}, f32[4]{0:T(128)S(1)}) all-reduce(f32[4,128]{1,0:T(4,128)S(1)} %fusion.15, f32[4]{0:T(128)S(1)} %get-tuple-element.13), channel_id=1, replica_groups=mesh['cluster'=8,'sub'=4] {'cluster','sub'}, use_global_device_ids=true, to_apply=%region_13.17 | all-reduce | flops 516 | bytes 4128 | tf_op jit(solution)/shard_map/psum | solution.py:73
  206.2 0.2 fusion.1
  206.4 7.2 %all-reduce.2 = (f32[4,384]{1,0:T(4,128)S(1)}, f32[4,128]{1,0:T(4,128)S(1)}) all-reduce(f32[4,384]{1,0:T(4,128)S(1)} %fusion.1, f32[4,128]{1,0:T(4,128)S(1)} %fusion.44), channel_id=1, replica_groups=mesh['cluster'=8,'sub'=4] {'sub'}, use_global_device_ids=true, to_apply=%region_12.16 | all-reduce | flops 2048 | bytes 16384 | tf_op jit(solution)/shard_map/psum | solution.py:78
  213.8 0.2 convolution_subtract_fusion.1
  214.1 0.6 gather_fusion.9
  214.7 0.3 fusion
  215.2 1.9 gather_fusion.12
  217.2 1.3 collective-permute-start.10
  218.7 1.9 gather_fusion.13
  220.6 4.0 %collective-permute-start.11 = (f32[1,2,4,128]{3,2,1,0:T(4,128)S(1)}, f32[1,2,4,128]{3,2,1,0:T(4,128)S(1)}, u32[]{:S(2)}, u32[]{:S(2)}) collective-permute-start(f32[1,2,4,128]{3,2,1,0:T(4,128)S(1)} %select_bitcast_fusion.2), channel_id=1, source_target_pairs={{0,4},{4,8},{8,12},{12,16},{16,20},{20,24},{24,28},{1,5},{5,9},{9,... | collective-permute-start | bytes 12296 | tf_op jit(solution)/shard_map/ppermute | solution.py:15
  224.8 3.7 %gather_fusion.10 = f32[512,4]{1,0:T(8,128)S(1)} fusion(f32[4,4,128]{1,2,0:T(8,128)S(1)} %copy.71, s32[512]{0:T(512)S(1)} %get-tuple-element.39), kind=kCustom, calls=%fused_computation.7.clone | custom fusion | bytes 20480 | tf_op jit(solution)/shard_map/jit(take_along_axis)/gather | solution.py:30
  228.6 3.3 %collective-permute-start.8 = (f32[1,4,4,128]{3,2,1,0:T(4,128)S(1)}, f32[1,4,4,128]{3,2,1,0:T(4,128)S(1)}, u32[]{:S(2)}, u32[]{:S(2)}) collective-permute-start(f32[1,4,4,128]{3,2,1,0:T(4,128)S(1)} %fusion.24), channel_id=1, source_target_pairs={{1,0},{2,1},{3,2},{5,4},{6,5},{7,6},{9,8},{10,9},{11,10},{13,12},{... | collective-permute-start | bytes 24584 | tf_op jit(solution)/shard_map/ppermute | solution.py:18
  232.0 3.7 %gather_fusion.11 = f32[512,4]{1,0:T(8,128)S(1)} fusion(f32[4,4,128]{1,2,0:T(8,128)S(1)} %copy.73, s32[512]{0:T(512)S(1)} %fusion.40), kind=kCustom, calls=%fused_computation.8.clone | custom fusion | bytes 20480 | tf_op jit(solution)/shard_map/jit(take_along_axis)/gather | solution.py:30
  235.8 3.1 %collective-permute-start.9 = (f32[1,4,4,128]{3,2,1,0:T(4,128)S(1)}, f32[1,4,4,128]{3,2,1,0:T(4,128)S(1)}, u32[]{:S(2)}, u32[]{:S(2)}) collective-permute-start(f32[1,4,4,128]{3,2,1,0:T(4,128)S(1)} %fusion.23), channel_id=1, source_target_pairs={{0,1},{1,2},{2,3},{4,5},{5,6},{6,7},{8,9},{9,10},{10,11},{12,13},{... | collective-permute-start | bytes 24584 | tf_op jit(solution)/shard_map/ppermute | solution.py:15
  239.0 0.7 collective-permute-done.9
  239.7 0.4 broadcast_multiply_fusion
  240.1 6.1 %psum.94 = f32[4]{0:T(128)S(1)} all-reduce(f32[4]{0:T(128)S(1)} %get-tuple-element.16), channel_id=1, replica_groups=mesh['cluster'=8,'sub'=4] {'sub'}, use_global_device_ids=true, to_apply=%region_16.20 | all-reduce | flops 4 | bytes 32 | tf_op jit(solution)/shard_map/psum | solution.py:54
  246.2 15.8 %psum.95 = f32[4]{0:T(128)S(1)} all-reduce(f32[4]{0:T(128)S(1)} %psum.94), channel_id=1, replica_groups=mesh['cluster'=8,'sub'=4] {'cluster'}, use_global_device_ids=true, to_apply=%region_17.21 | all-reduce | flops 4 | bytes 32 | tf_op jit(solution)/shard_map/psum | solution.py:54
  262.2 1.9 gather_fusion.16
  264.2 1.5 collective-permute-start.14
  265.8 1.9 gather_fusion.17
  267.8 4.0 %collective-permute-start.15 = (f32[1,2,4,128]{3,2,1,0:T(4,128)S(1)}, f32[1,2,4,128]{3,2,1,0:T(4,128)S(1)}, u32[]{:S(2)}, u32[]{:S(2)}) collective-permute-start(f32[1,2,4,128]{3,2,1,0:T(4,128)S(1)} %select_bitcast_fusion), channel_id=1, source_target_pairs={{0,4},{4,8},{8,12},{12,16},{16,20},{20,24},{24,28},{1,5},{5,9},{9,... | collective-permute-start | bytes 12296 | tf_op jit(solution)/shard_map/ppermute | solution.py:15
  272.0 3.7 %gather_fusion.14 = f32[512,4]{1,0:T(8,128)S(1)} fusion(f32[4,4,128]{1,2,0:T(8,128)S(1)} %copy.79, s32[512]{0:T(512)S(1)} %get-tuple-element.39), kind=kCustom, calls=%fused_computation.9.clone | custom fusion | bytes 20480 | tf_op jit(solution)/shard_map/jit(take_along_axis)/gather | solution.py:30
  275.8 6.7 %collective-permute-start.12 = (f32[1,4,4,128]{3,2,1,0:T(4,128)S(1)}, f32[1,4,4,128]{3,2,1,0:T(4,128)S(1)}, u32[]{:S(2)}, u32[]{:S(2)}) collective-permute-start(f32[1,4,4,128]{3,2,1,0:T(4,128)S(1)} %fusion.22), channel_id=1, source_target_pairs={{1,0},{2,1},{3,2},{5,4},{6,5},{7,6},{9,8},{10,9},{11,10},{13,12},{... | collective-permute-start | bytes 24584 | tf_op jit(solution)/shard_map/ppermute | solution.py:18
  282.6 3.7 %gather_fusion.15 = f32[512,4]{1,0:T(8,128)S(1)} fusion(f32[4,4,128]{1,2,0:T(8,128)S(1)} %copy.81, s32[512]{0:T(512)S(1)} %fusion.40), kind=kCustom, calls=%fused_computation.10.clone | custom fusion | bytes 20480 | tf_op jit(solution)/shard_map/jit(take_along_axis)/gather | solution.py:30
  286.4 3.4 %collective-permute-start.13 = (f32[1,4,4,128]{3,2,1,0:T(4,128)S(1)}, f32[1,4,4,128]{3,2,1,0:T(4,128)S(1)}, u32[]{:S(2)}, u32[]{:S(2)}) collective-permute-start(f32[1,4,4,128]{3,2,1,0:T(4,128)S(1)} %fusion.21), channel_id=1, source_target_pairs={{0,1},{1,2},{2,3},{4,5},{5,6},{6,7},{8,9},{9,10},{10,11},{12,13},{... | collective-permute-start | bytes 24584 | tf_op jit(solution)/shard_map/ppermute | solution.py:15
  289.9 0.7 collective-permute-done.13
  290.6 0.7 fusion.10
  (128 shorter events, 6.0 us)
Async XLA Ops:
  0.6 116.8 %copy-start = (bf16[4,384,384]{2,1,0:T(8,128)(2,1)S(1)}, bf16[4,384,384]{2,1,0:T(8,128)(2,1)}, u32[]{:S(2)}) copy-start(bf16[4,384,384]{2,1,0:T(8,128)(2,1)} %param.16) | copy-start | bytes 3538948
  0.6 61.4 %copy-start.6 = (s32[4,3,128]{2,0,1:T(4,128)S(1)}, s32[4,3,128]{2,0,1:T(4,128)}, u32[]{:S(2)}) copy-start(s32[4,3,128]{2,0,1:T(4,128)} %param.18) | copy-start | bytes 18436
  60.7 56.0 %collective-permute-start.2 = (f32[1,2,4,128]{3,2,1,0:T(4,128)S(1)}, f32[1,2,4,128]{3,2,1,0:T(4,128)S(1)}, u32[]{:S(2)}, u32[]{:S(2)}) collective-permute-start(f32[1,2,4,128]{3,2,1,0:T(4,128)S(1)} %select_bitcast_fusion.7), channel_id=1, source_target_pairs={{4,0},{8,4},{12,8},{16,12},{20,16},{24,20},{28,24},{5,1},{9,5},{13... | collective-permute-start | bytes 12296 | tf_op jit(solution)/shard_map/ppermute | solution.py:18
  75.7 41.0 %collective-permute-start.3 = (f32[1,2,4,128]{3,2,1,0:T(4,128)S(1)}, f32[1,2,4,128]{3,2,1,0:T(4,128)S(1)}, u32[]{:S(2)}, u32[]{:S(2)}) collective-permute-start(f32[1,2,4,128]{3,2,1,0:T(4,128)S(1)} %select_bitcast_fusion.6), channel_id=1, source_target_pairs={{0,4},{4,8},{8,12},{12,16},{16,20},{20,24},{24,28},{1,5},{5,9},{9,... | collective-permute-start | bytes 12296 | tf_op jit(solution)/shard_map/ppermute | solution.py:15
  83.7 33.0 %collective-permute-start = (f32[1,4,4,128]{3,2,1,0:T(4,128)S(1)}, f32[1,4,4,128]{3,2,1,0:T(4,128)S(1)}, u32[]{:S(2)}, u32[]{:S(2)}) collective-permute-start(f32[1,4,4,128]{3,2,1,0:T(4,128)S(1)} %fusion.28), channel_id=1, source_target_pairs={{1,0},{2,1},{3,2},{5,4},{6,5},{7,6},{9,8},{10,9},{11,10},{13,12},{... | collective-permute-start | bytes 24584 | tf_op jit(solution)/shard_map/ppermute | solution.py:18
  86.8 29.9 %copy-start.7 = (s32[4,384]{1,0:T(4,128)S(1)}, s32[4,384]{1,0:T(4,128)}, u32[]{:S(2)}) copy-start(s32[4,384]{1,0:T(4,128)} %param.17) | copy-start | bytes 18436
  113.3 4.1 %collective-permute-start.1 = (f32[1,4,4,128]{3,2,1,0:T(4,128)S(1)}, f32[1,4,4,128]{3,2,1,0:T(4,128)S(1)}, u32[]{:S(2)}, u32[]{:S(2)}) collective-permute-start(f32[1,4,4,128]{3,2,1,0:T(4,128)S(1)} %fusion.27), channel_id=1, source_target_pairs={{0,1},{1,2},{2,3},{4,5},{5,6},{6,7},{8,9},{9,10},{10,11},{12,13},{... | collective-permute-start | bytes 24584 | tf_op jit(solution)/shard_map/ppermute | solution.py:15
  141.6 26.1 %copy-start.3 = (f32[4,4,384]{2,1,0:T(4,128)S(1)}, f32[4,4,384]{2,1,0:T(4,128)}, u32[]{:S(2)}) copy-start(f32[4,4,384]{2,1,0:T(4,128)} %param.15) | copy-start | bytes 73732
  141.7 25.2 %collective-permute-start.6 = (f32[1,2,4,128]{3,2,1,0:T(4,128)S(1)}, f32[1,2,4,128]{3,2,1,0:T(4,128)S(1)}, u32[]{:S(2)}, u32[]{:S(2)}) collective-permute-start(f32[1,2,4,128]{3,2,1,0:T(4,128)S(1)} %select_bitcast_fusion.5), channel_id=1, source_target_pairs={{4,0},{8,4},{12,8},{16,12},{20,16},{24,20},{28,24},{5,1},{9,5},{13... | collective-permute-start | bytes 12296 | tf_op jit(solution)/shard_map/ppermute | solution.py:18
  143.0 24.9 %copy-start.2 = (f32[4,8,384]{2,1,0:T(8,128)S(1)}, f32[4,8,384]{2,1,0:T(8,128)}, u32[]{:S(2)}) copy-start(f32[4,8,384]{2,1,0:T(8,128)} %param.20) | copy-start | bytes 147460
  143.1 24.9 %copy-start.1 = (f32[4,24,384]{2,1,0:T(8,128)S(1)}, f32[4,24,384]{2,1,0:T(8,128)}, u32[]{:S(2)}) copy-start(f32[4,24,384]{2,1,0:T(8,128)} %param.19) | copy-start | bytes 442372
  145.0 60.9 %copy-start.5 = (f32[32,128]{1,0:T(8,128)S(1)}, f32[32,128]{1,0:T(8,128)}, u32[]{:S(2)}) copy-start(f32[32,128]{1,0:T(8,128)} %param.23) | copy-start | bytes 49156
  145.1 61.1 %copy-start.4 = (f32[1,96,384]{2,1,0:T(8,128)S(1)}, f32[1,96,384]{2,1,0:T(8,128)}, u32[]{:S(2)}) copy-start(f32[1,96,384]{2,1,0:T(8,128)} %param.22) | copy-start | bytes 442372
  145.1 21.8 %collective-permute-start.7 = (f32[1,2,4,128]{3,2,1,0:T(4,128)S(1)}, f32[1,2,4,128]{3,2,1,0:T(4,128)S(1)}, u32[]{:S(2)}, u32[]{:S(2)}) collective-permute-start(f32[1,2,4,128]{3,2,1,0:T(4,128)S(1)} %select_bitcast_fusion.4), channel_id=1, source_target_pairs={{0,4},{4,8},{8,12},{12,16},{16,20},{20,24},{24,28},{1,5},{5,9},{9,... | collective-permute-start | bytes 12296 | tf_op jit(solution)/shard_map/ppermute | solution.py:15
  153.4 13.6 %collective-permute-start.4 = (f32[1,4,4,128]{3,2,1,0:T(4,128)S(1)}, f32[1,4,4,128]{3,2,1,0:T(4,128)S(1)}, u32[]{:S(2)}, u32[]{:S(2)}) collective-permute-start(f32[1,4,4,128]{3,2,1,0:T(4,128)S(1)} %fusion.26), channel_id=1, source_target_pairs={{1,0},{2,1},{3,2},{5,4},{6,5},{7,6},{9,8},{10,9},{11,10},{13,12},{... | collective-permute-start | bytes 24584 | tf_op jit(solution)/shard_map/ppermute | solution.py:18
  163.3 4.4 %collective-permute-start.5 = (f32[1,4,4,128]{3,2,1,0:T(4,128)S(1)}, f32[1,4,4,128]{3,2,1,0:T(4,128)S(1)}, u32[]{:S(2)}, u32[]{:S(2)}) collective-permute-start(f32[1,4,4,128]{3,2,1,0:T(4,128)S(1)} %fusion.25), channel_id=1, source_target_pairs={{0,1},{1,2},{2,3},{4,5},{5,6},{6,7},{8,9},{9,10},{10,11},{12,13},{... | collective-permute-start | bytes 24584 | tf_op jit(solution)/shard_map/ppermute | solution.py:15
  217.2 21.7 %collective-permute-start.10 = (f32[1,2,4,128]{3,2,1,0:T(4,128)S(1)}, f32[1,2,4,128]{3,2,1,0:T(4,128)S(1)}, u32[]{:S(2)}, u32[]{:S(2)}) collective-permute-start(f32[1,2,4,128]{3,2,1,0:T(4,128)S(1)} %select_bitcast_fusion.3), channel_id=1, source_target_pairs={{4,0},{8,4},{12,8},{16,12},{20,16},{24,20},{28,24},{5,1},{9,5},{13... | collective-permute-start | bytes 12296 | tf_op jit(solution)/shard_map/ppermute | solution.py:18
  220.6 18.3 %collective-permute-start.11 = (f32[1,2,4,128]{3,2,1,0:T(4,128)S(1)}, f32[1,2,4,128]{3,2,1,0:T(4,128)S(1)}, u32[]{:S(2)}, u32[]{:S(2)}) collective-permute-start(f32[1,2,4,128]{3,2,1,0:T(4,128)S(1)} %select_bitcast_fusion.2), channel_id=1, source_target_pairs={{0,4},{4,8},{8,12},{12,16},{16,20},{20,24},{24,28},{1,5},{5,9},{9,... | collective-permute-start | bytes 12296 | tf_op jit(solution)/shard_map/ppermute | solution.py:15
  228.6 10.4 %collective-permute-start.8 = (f32[1,4,4,128]{3,2,1,0:T(4,128)S(1)}, f32[1,4,4,128]{3,2,1,0:T(4,128)S(1)}, u32[]{:S(2)}, u32[]{:S(2)}) collective-permute-start(f32[1,4,4,128]{3,2,1,0:T(4,128)S(1)} %fusion.24), channel_id=1, source_target_pairs={{1,0},{2,1},{3,2},{5,4},{6,5},{7,6},{9,8},{10,9},{11,10},{13,12},{... | collective-permute-start | bytes 24584 | tf_op jit(solution)/shard_map/ppermute | solution.py:18
  235.8 3.9 %collective-permute-start.9 = (f32[1,4,4,128]{3,2,1,0:T(4,128)S(1)}, f32[1,4,4,128]{3,2,1,0:T(4,128)S(1)}, u32[]{:S(2)}, u32[]{:S(2)}) collective-permute-start(f32[1,4,4,128]{3,2,1,0:T(4,128)S(1)} %fusion.23), channel_id=1, source_target_pairs={{0,1},{1,2},{2,3},{4,5},{5,6},{6,7},{8,9},{9,10},{10,11},{12,13},{... | collective-permute-start | bytes 24584 | tf_op jit(solution)/shard_map/ppermute | solution.py:15
  264.2 25.7 %collective-permute-start.14 = (f32[1,2,4,128]{3,2,1,0:T(4,128)S(1)}, f32[1,2,4,128]{3,2,1,0:T(4,128)S(1)}, u32[]{:S(2)}, u32[]{:S(2)}) collective-permute-start(f32[1,2,4,128]{3,2,1,0:T(4,128)S(1)} %select_bitcast_fusion.1), channel_id=1, source_target_pairs={{4,0},{8,4},{12,8},{16,12},{20,16},{24,20},{28,24},{5,1},{9,5},{13... | collective-permute-start | bytes 12296 | tf_op jit(solution)/shard_map/ppermute | solution.py:18
  267.8 22.0 %collective-permute-start.15 = (f32[1,2,4,128]{3,2,1,0:T(4,128)S(1)}, f32[1,2,4,128]{3,2,1,0:T(4,128)S(1)}, u32[]{:S(2)}, u32[]{:S(2)}) collective-permute-start(f32[1,2,4,128]{3,2,1,0:T(4,128)S(1)} %select_bitcast_fusion), channel_id=1, source_target_pairs={{0,4},{4,8},{8,12},{12,16},{16,20},{20,24},{24,28},{1,5},{5,9},{9,... | collective-permute-start | bytes 12296 | tf_op jit(solution)/shard_map/ppermute | solution.py:15
  275.8 14.1 %collective-permute-start.12 = (f32[1,4,4,128]{3,2,1,0:T(4,128)S(1)}, f32[1,4,4,128]{3,2,1,0:T(4,128)S(1)}, u32[]{:S(2)}, u32[]{:S(2)}) collective-permute-start(f32[1,4,4,128]{3,2,1,0:T(4,128)S(1)} %fusion.22), channel_id=1, source_target_pairs={{1,0},{2,1},{3,2},{5,4},{6,5},{7,6},{9,8},{10,9},{11,10},{13,12},{... | collective-permute-start | bytes 24584 | tf_op jit(solution)/shard_map/ppermute | solution.py:18
  286.4 4.2 %collective-permute-start.13 = (f32[1,4,4,128]{3,2,1,0:T(4,128)S(1)}, f32[1,4,4,128]{3,2,1,0:T(4,128)S(1)}, u32[]{:S(2)}, u32[]{:S(2)}) collective-permute-start(f32[1,4,4,128]{3,2,1,0:T(4,128)S(1)} %fusion.21), channel_id=1, source_target_pairs={{0,1},{1,2},{2,3},{4,5},{5,6},{6,7},{8,9},{9,10},{10,11},{12,13},{... | collective-permute-start | bytes 24584 | tf_op jit(solution)/shard_map/ppermute | solution.py:15
